TPU v7x, 256 devices: a whole 4x4x8 slice. The times are simulated.
256 devices in a mesh: grp: 64 (over z_lo, x, y), sub: 4 (over z_hi, core).
Axes of the slice: x: 4, y: 4, z: 8 (z_hi: 2, z_lo: 4; z = z_hi * 4 + z_lo), core: 2. Of those that a mesh axis runs over, the one named last changes fastest.
Arguments:
- blocks: bfloat16 [2048, 128, 128], P(('grp', 'sub')), may hold values from -0.5 to 0.5
- block_cols: int32 [2048], P(('grp', 'sub')), may hold values from 0 to 255, as said below
- far_slots: int32 [256, 256], P(('grp', 'sub')), may hold values from 0 to 7, as said below
- pair_lists: int32 [256, 4, 1024], P(('grp', 'sub')), may hold values from 0 to 7, as said below
Outputs:
- participation: float32 [32768], P(('grp', 'sub'))
- total: float32 [], replicated
Inputs may be any that keep to these rules, and one draw needn't show every extreme that they name: `block_cols`: the block column of slot t is at most its block row t // 8. `far_slots`: the 4 slots of one block row and source group are distinct. `pair_lists`: rows 0 and 2 hold slot numbers below 8, row 1 positions below 4, row 3 holds 0 or 1; within one block row and source group no two triples share both their left slot and far position.
All inputs are finite; a program needn't handle non-finite values.
Results may differ from a plain program's by a relative error of at most 0.00035.
Values may be sent and summed in bfloat16 or wider, within the bound.
A program may use at most 64 MiB of HBM per device.

v0:
```python
import math

import jax
import jax.numpy as jnp
from jax import lax
from jax.sharding import Mesh
from jax.sharding import PartitionSpec as P

GRP = ("grp_0", "grp_1", "grp_2")
SUB = ("sub_0", "sub_1")
GRP_SUB = ("grp_0", "grp_1", "grp_2", "sub_0", "sub_1")


def by_axis(value, axes):
    for axis in axes:
        value = lax.psum(value, axis)
    return value


def select_rows(indices, table):
    choices_of = (indices[:, None] == jnp.arange(table.shape[0], dtype=jnp.int32)[None, :]).astype(
        table.dtype
    )
    return jnp.dot(choices_of, table, preferred_element_type=jnp.float32).astype(table.dtype)


def triple_sums(left, far, mask, live, size):
    count = left.shape[0]
    left_blocks = left.reshape(count, size, size)
    far_blocks = far.reshape(count, size, size)
    mask_blocks = mask.reshape(count, size, size)
    product = jnp.einsum(
        "wik,wkj->wij", left_blocks, far_blocks, preferred_element_type=jnp.float32
    )
    sums = jnp.sum(mask_blocks.astype(jnp.float32) * product, axis=2)
    return jnp.dot(live.astype(jnp.float32), sums, precision=lax.Precision.HIGHEST)


def local(blocks, block_cols, far_slots, pair_lists):
    stored = blocks.shape[0]
    size = blocks.shape[1]
    groups = lax.axis_size(GRP)
    subs = lax.axis_size(SUB)
    myself = lax.axis_index(GRP_SUB)
    inner = jnp.arange(size, dtype=jnp.int32)
    strict = inner[:, None] > inner[None, :]
    on_diag = block_cols == myself
    own = jnp.where(
        on_diag[:, None, None] & jnp.logical_not(strict)[None], jnp.zeros((), blocks.dtype), blocks
    )
    own_flat = own.reshape(stored, size * size)
    lists = pair_lists[0]
    per_source = lists.shape[1] // groups
    left_idx = lists[0].reshape(groups, per_source)
    far_idx = lists[1].reshape(groups, per_source)
    mask_idx = lists[2].reshape(groups, per_source)
    live_idx = lists[3].reshape(groups, per_source)
    wanted_row = far_slots[0].reshape(groups, far_slots.shape[1] // groups)
    requests = lax.all_to_all(wanted_row, GRP, split_axis=0, concat_axis=0, tiled=True)
    outgoing = jax.vmap(lambda wanted: select_rows(wanted, own_flat))(requests)
    fetched = lax.all_to_all(outgoing, GRP, split_axis=0, concat_axis=0, tiled=True)

    def one_source(running, item):
        chosen, left_slot, far_place, mask_slot, live = item
        far = select_rows(far_place, chosen)
        left = select_rows(left_slot, own_flat)
        mask = select_rows(mask_slot, own_flat)
        return (running + triple_sums(left, far, mask, live, size), None)

    participation, unused = lax.scan(
        one_source,
        jnp.zeros((size,), jnp.float32),
        (fetched, left_idx, far_idx, mask_idx, live_idx),
    )
    summed = by_axis(jnp.sum(participation), GRP_SUB)
    total = summed / math.sqrt(groups * subs * size)
    return (participation, total)


def solution(mesh):
    torus = Mesh(mesh.devices.reshape(4, 4, 4, 2, 2), ("grp_0", "grp_1", "grp_2", "sub_0", "sub_1"))
    in_specs = (P(GRP_SUB, None, None), P(GRP_SUB), P(GRP_SUB, None), P(GRP_SUB, None, None))
    out_specs = (P(GRP_SUB), P())
    return jax.shard_map(local, mesh=torus, in_specs=in_specs, out_specs=out_specs, check_vma=False)
```

profile of v0, /device:TPU:1, one launch (start us, length us, event | category | flops | bytes accessed | tf_op | source)
XLA Modules:
  0.0 505.5 jit_solution(7977299324315457463)
XLA Ops:
  1.1 1.3 reduce.19
  3.2 12.5 %all-to-all-start = ((s32[64,1,4]{2,1,0:T(1,128)}), s32[64,1,4]{2,1,0:T(1,128)S(1)}, u32[]{:S(2)}, u32[]{:S(2)}) async-start(s32[64,1,4]{2,1,0:T(1,128)} %bitcast), calls=%async_computation | async-start | bytes 65536 | tf_op jit(solution)/shard_map/all_to_all | solution.py:59
  17.7 7.1 %all-to-all-done = s32[64,1,4]{2,1,0:T(1,128)S(1)} async-done(((s32[64,1,4]{2,1,0:T(1,128)}), s32[64,1,4]{2,1,0:T(1,128)S(1)}, u32[]{:S(2)}, u32[]{:S(2)}) %all-to-all-start) | async-done | bytes 1056 | tf_op jit(solution)/shard_map/all_to_all | solution.py:59
  24.8 2.4 convolution_convert_fusion.3
  27.2 17.2 %copy.14 = bf16[64,4,16384]{2,1,0:T(4,128)(2,1)} copy(bf16[64,4,16384]{2,0,1:T(8,128)(2,1)S(1)} %convolution_convert_fusion.3) | data formatting | bytes 16777216 | tf_op jit(solution)/shard_map/vmap()/convert_element_type | solution.py:24
  44.4 5.9 %all-to-all-start.1 = ((bf16[64,4,16384]{2,1,0:T(4,128)(2,1)}), bf16[64,4,16384]{2,1,0:T(4,128)(2,1)}, u32[]{:S(2)}, u32[]{:S(2)}) async-start(bf16[64,4,16384]{2,1,0:T(4,128)(2,1)} %copy.14), calls=%async_computation.1 | async-start | bytes 16777216 | tf_op jit(solution)/shard_map/all_to_all | solution.py:61
  51.0 184.8 %all-to-all-done.1 = bf16[64,4,16384]{2,1,0:T(4,128)(2,1)} async-done(((bf16[64,4,16384]{2,1,0:T(4,128)(2,1)}), bf16[64,4,16384]{2,1,0:T(4,128)(2,1)}, u32[]{:S(2)}, u32[]{:S(2)}) %all-to-all-start.1) | async-done | bytes 8388640 | tf_op jit(solution)/shard_map/all_to_all | solution.py:61
  235.8 218.8 %while.11 = (s32[]{:T(128)}, f32[128]{0:T(128)S(1)}, s32[64,16]{1,0:T(8,128)S(1)}, s32[64,16]{1,0:T(8,128)S(1)}, bf16[8,16384]{1,0:T(8,128)(2,1)S(1)}, /*index=5...) while((s32[]{:T(128)}, f32[128]{0:T(128)S(1)}, ...), condition=%wide.region_2.3_spmd.clone, body=%wide.region_0.2_spmd.clone.sunk | while | flops 79190608 | bytes 11160251 | solution.py:70
  239.2 1.3 fusion.52
  242.6 1.3 fusion.52
  246.1 1.3 fusion.52
  249.5 1.3 fusion.52
  252.9 1.3 fusion.52
  256.3 1.3 fusion.52
  259.7 1.3 fusion.52
  263.2 1.3 fusion.52
  266.6 1.3 fusion.52
  270.0 1.3 fusion.52
  273.4 1.3 fusion.52
  276.8 1.3 fusion.52
  283.7 1.3 fusion.52
  287.1 1.3 fusion.52
  290.5 1.3 fusion.52
  293.9 1.3 fusion.52
  297.3 1.3 fusion.52
  300.8 1.3 fusion.52
  304.2 1.3 fusion.52
  307.6 1.3 fusion.52
  311.0 1.3 fusion.52
  314.4 1.3 fusion.52
  317.9 1.3 fusion.52
  321.3 1.3 fusion.52
  324.7 1.3 fusion.52
  328.1 1.3 fusion.52
  331.5 1.3 fusion.52
  335.0 1.3 fusion.52
  338.4 1.3 fusion.52
  341.8 1.3 fusion.52
  348.6 1.3 fusion.52
  352.0 1.3 fusion.52
  355.5 1.3 fusion.52
  358.9 1.3 fusion.52
  362.3 1.3 fusion.52
  455.2 8.0 %psum.35 = f32[]{:T(128)} all-reduce(f32[]{:T(128)} %reduce_sum.18), channel_id=1, replica_groups=mesh['grp_0'=4,'grp_1'=4,'grp_2'=4,'sub_0'=2,'sub_1'=2] {'grp_0'}, use_global_device_ids=true, to_apply=%region_4.5 | all-reduce | flops 1 | bytes 8 | tf_op jit(solution)/shard_map/psum | solution.py:16
  463.2 8.9 %psum.36 = f32[]{:T(128)} all-reduce(f32[]{:T(128)} %psum.35), channel_id=1, replica_groups=mesh['grp_0'=4,'grp_1'=4,'grp_2'=4,'sub_0'=2,'sub_1'=2] {'grp_1'}, use_global_device_ids=true, to_apply=%region_5.6 | all-reduce | flops 1 | bytes 8 | tf_op jit(solution)/shard_map/psum | solution.py:16
  472.0 11.8 %psum.37 = f32[]{:T(128)} all-reduce(f32[]{:T(128)} %psum.36), channel_id=1, replica_groups=mesh['grp_0'=4,'grp_1'=4,'grp_2'=4,'sub_0'=2,'sub_1'=2] {'grp_2'}, use_global_device_ids=true, to_apply=%region_6.7 | all-reduce | flops 1 | bytes 8 | tf_op jit(solution)/shard_map/psum | solution.py:16
  483.8 8.3 %psum.38 = f32[]{:T(128)} all-reduce(f32[]{:T(128)} %psum.37), channel_id=1, replica_groups=mesh['grp_0'=4,'grp_1'=4,'grp_2'=4,'sub_0'=2,'sub_1'=2] {'sub_0'}, use_global_device_ids=true, to_apply=%region_7.8 | all-reduce | flops 1 | bytes 8 | tf_op jit(solution)/shard_map/psum | solution.py:16
  492.1 11.5 %psum.39 = f32[]{:T(128)} all-reduce(f32[]{:T(128)} %psum.38), channel_id=1, replica_groups=mesh['grp_0'=4,'grp_1'=4,'grp_2'=4,'sub_0'=2,'sub_1'=2] {'sub_1'}, use_global_device_ids=true, to_apply=%region_8.9 | all-reduce | flops 1 | bytes 8 | tf_op jit(solution)/shard_map/psum | solution.py:16
  (691 shorter events, 174.8 us)
Async XLA Ops:
  3.2 21.6 %all-to-all-start = ((s32[64,1,4]{2,1,0:T(1,128)}), s32[64,1,4]{2,1,0:T(1,128)S(1)}, u32[]{:S(2)}, u32[]{:S(2)}) async-start(s32[64,1,4]{2,1,0:T(1,128)} %bitcast), calls=%async_computation | async-start | bytes 65536 | tf_op jit(solution)/shard_map/all_to_all | solution.py:59
  44.4 5.9 %copy-start = (bf16[8,128,128]{2,1,0:T(8,128)(2,1)S(1)}, bf16[8,128,128]{2,1,0:T(8,128)(2,1)}, u32[]{:S(2)}) copy-start(bf16[8,128,128]{2,1,0:T(8,128)(2,1)} %param.6) | copy-start | bytes 786436
  44.4 6.3 %copy-start.1 = (s32[1,4,1024]{2,1,0:T(4,128)S(1)}, s32[1,4,1024]{2,1,0:T(4,128)}, u32[]{:S(2)}) copy-start(s32[1,4,1024]{2,1,0:T(4,128)} %param.9) | copy-start | bytes 49156
  44.4 191.4 %all-to-all-start.1 = ((bf16[64,4,16384]{2,1,0:T(4,128)(2,1)}), bf16[64,4,16384]{2,1,0:T(4,128)(2,1)}, u32[]{:S(2)}, u32[]{:S(2)}) async-start(bf16[64,4,16384]{2,1,0:T(4,128)(2,1)} %copy.14), calls=%async_computation.1 | async-start | bytes 16777216 | tf_op jit(solution)/shard_map/all_to_all | solution.py:61
  454.6 49.7 %copy-start.2 = (f32[128]{0:T(128)}, f32[128]{0:T(128)S(1)}, u32[]{:S(2)}) copy-start(f32[128]{0:T(128)S(1)} %get-tuple-element.42) | copy-start | bytes 1540
where the time goes:
time: 507 us; the launch traced here: 505 us
  waiting for transfers between devices  192 us (38%)
  matrix products  169 us (33%)
  local copies, waits for them, and re-layouts  66.3 us (13%)
  blocking collectives  48.5 us (10%)
  starting transfers between devices  18.4 us (4%)
    all_to_all x1, waiting for transfers between devices, local(): lax.all_to_all(outgoing, GRP, split_axis=0, concat_axis=0, tiled=True)  185 us
    dot_general x193, matrix products, select_rows(): jnp.dot(choices_of, table, preferred_element_type=jnp.float32)  127 us
    psum x5, blocking collectives, by_axis(): value = lax.psum(value, axis)  48.5 us
    dot_general x64, matrix products, triple_sums(): jnp.einsum('wik,wkj->wij', left_blocks, far_blocks, preferred_element_typ...  33.8 us
    while x192, local copies, waits for them, and re-layouts  24.8 us
    convert_element_type x64, local copies, waits for them, and re-layouts, triple_sums(): sums = jnp.sum(mask_blocks.astype(jnp.float32) * product, axis=2)  21.2 us
    convert_element_type x1, local copies, waits for them, and re-layouts, select_rows(): jnp.dot(choices_of, table, preferred_element_type=jnp.float32)  17.2 us
    all_to_all x1, starting transfers between devices, local(): lax.all_to_all(wanted_row, GRP, split_axis=0, concat_axis=0, tiled=True)  12.5 us
  transfers between devices with their start and end apart: 2, of which 2 were waited for; matrix products, arithmetic and copies ran while one was open for 1% of the time, Pallas kernels for 0%

commit v1 on v0

v1 whole, which is shorter than its diff:
```python
import functools
import math

import jax
import jax.numpy as jnp
from jax import lax
from jax.experimental import pallas as pl
from jax.experimental.pallas import tpu as pltpu
from jax.sharding import Mesh
from jax.sharding import PartitionSpec as P

GRP = ("grp_0", "grp_1", "grp_2")
SUB = ("sub_0", "sub_1")
GRP_SUB = GRP + SUB
MESH_IDS = pl.DeviceIdType.MESH
R, D, L = 1, 2, 3


def kernel(
    blocks_hbm, cols_ref, far_hbm, lists_hbm,
    part_ref, total_ref,
    raw, own, r_near, r_far, q_near, q_zown, q_far,
    lists_v, far_v, lists_own, far_own, lists_near, far_near, lists_far, far_far,
    accum, part_send, part_recv, plane_recv, depth_send, depth_recv,
    load_sem, smem_sem,
    send_r, recv_r, send_q, recv_q, send_l, recv_l, send_f, recv_f,
    send_p, recv_p, send_t, recv_t, send_d, recv_d,
):
    z = lax.axis_index("grp_0")
    x = lax.axis_index("grp_1")
    y = lax.axis_index("grp_2")
    zh = lax.axis_index("sub_0")
    core = lax.axis_index("sub_1")
    kd, size = blocks_hbm.shape[0], blocks_hbm.shape[1]
    half = kd // 2
    other = 1 - core

    def at(dz, dx, dy):
        return (dz, lax.rem(x + dx, 4), lax.rem(y + dy, 4), zh, core)

    def row_at(dz, step):
        return at(dz, core * step, other * step)

    def src_at(dz, step):
        return at(dz, other * step, core * step)

    z1 = z + 1 - 2 * lax.rem(z, 2)
    z2 = lax.rem(z + 2, 4)
    place = x * 4 + y
    level = (zh * 4 + z) * 2 + core

    def plane_dev(p):
        return (z, p // 4, lax.rem(p, 4), zh, core)

    def level_dev(p):
        return (lax.rem(p // 2, 4), x, y, p // 8, lax.rem(p, 2))

    barrier = pltpu.get_barrier_semaphore()

    def greet(dev):
        pl.semaphore_signal(barrier, inc=1, device_id=dev, device_id_type=MESH_IDS)

    load = pltpu.make_async_copy(blocks_hbm, raw, load_sem.at[0])
    load.start()
    own_lists = pltpu.make_async_copy(lists_hbm, lists_own.at[0], load_sem.at[1])
    own_lists.start()
    own_far = pltpu.make_async_copy(far_hbm, far_own.at[0], load_sem.at[2])
    own_far.start()

    def greet_both(k, carry):
        greet(plane_dev(lax.rem(place + k, 16)))
        greet(level_dev(lax.rem(level + k, 16)))
        return carry

    lax.fori_loop(1, 16, greet_both, 0)
    for step in (R, D, L):
        greet(row_at(z1, step))

    zero = jnp.zeros((size, size), jnp.bfloat16)
    own[kd] = zero
    for s in range(3):
        r_near[s, kd] = zero
    for s in range(4):
        r_far[s, kd] = zero
    for s in range(8):
        accum[s] = jnp.zeros((size, size), jnp.float32)
    load.wait()
    me = ((z * 4 + x) * 4 + y) * 4 + zh * 2 + core
    rows = lax.broadcasted_iota(jnp.int32, (size, size), 0)
    cols = lax.broadcasted_iota(jnp.int32, (size, size), 1)
    for t in range(kd):
        shift = jnp.where(cols_ref[t] == me, 0, size)
        block = raw[t].astype(jnp.float32)
        own[t] = jnp.where(rows + shift > cols, block, 0.0).astype(jnp.bfloat16)

    pl.semaphore_wait(barrier, 33)

    def remote(src, dst, ssem, rsem, dev):
        return pltpu.make_async_remote_copy(
            src_ref=src, dst_ref=dst, send_sem=ssem, recv_sem=rsem,
            device_id=dev, device_id_type=MESH_IDS,
        )

    mine = own.at[pl.ds(0, kd)]
    first, second = pl.ds(0, half), pl.ds(half, half)
    whole = pl.ds(0, kd)

    def slot_r(o):
        return r_near.at[o - 1] if o < 4 else r_far.at[o - 4]

    def slot_q(o):
        if o < 4:
            return q_near.at[o - 1]
        return q_zown if o == 4 else q_far.at[o - 5]

    def ring_copies(slot, near, dev, base, ssem, rsem):
        zz = base
        return {
            "L": remote(near, slot(zz + L).at[whole], ssem.at[zz + 0], rsem.at[zz + 0], dev(z, 1)),
            "R": remote(near, slot(zz + R).at[whole], ssem.at[zz + 1], rsem.at[zz + 1], dev(z, 3)),
            "D1": remote(slot(zz + L).at[first], slot(zz + D).at[first], ssem.at[zz + 2], rsem.at[zz + 2], dev(z, 1)),
            "D2": remote(slot(zz + R).at[second], slot(zz + D).at[second], ssem.at[zz + 3], rsem.at[zz + 3], dev(z, 3)),
        }

    rn = ring_copies(slot_r, mine, row_at, 0, send_r, recv_r)
    qn = ring_copies(slot_q, mine, src_at, 0, send_q, recv_q)
    rf = ring_copies(slot_r, slot_r(4).at[whole], row_at, 4, send_r, recv_r)
    qf = ring_copies(slot_q, slot_q(4).at[whole], src_at, 4, send_q, recv_q)
    rz = remote(mine, slot_r(4).at[whole], send_r.at[8], recv_r.at[8], row_at(z1, 0))
    qz = remote(mine, slot_q(4).at[whole], send_q.at[8], recv_q.at[8], src_at(z2, 0))

    for copy in (rz, rn["L"], rn["R"], qn["L"], qn["R"], qz):
        copy.start()

    back = {0: 0, R: L, D: D, L: R}
    list_copies = []
    for o in range(1, 8):
        dev = row_at(z if o < 4 else z1, o % 4)
        there = (o // 4) * 4 + back[o % 4]
        list_copies.append(remote(lists_hbm, lists_v.at[there], send_l.at[o], recv_l.at[there], dev))
        list_copies.append(remote(far_hbm, far_v.at[there], send_f.at[o], recv_f.at[there], dev))
    for copy in list_copies:
        copy.start()
    own_lists.wait()
    own_far.wait()

    ub = x + core * (y - x)
    ua = y + core * (x - y)

    def source_group(o):
        b = lax.rem(ub + o, 4)
        zq = z if o < 4 else z2
        xq = b + core * (ua - b)
        yq = ua + core * (b - ua)
        return zq * 16 + xq * 4 + yq

    def triples(row_ref, lists, fars, rr, q_ref, q_index, group, acc):
        base = group * 16

        def pick(w):
            left = lists[rr, 0, base + w]
            far = fars[rr, 0, group * 4 + lists[rr, 1, base + w]]
            mask = lists[rr, 2, base + w]
            left = jnp.where(lists[rr, 3, base + w] > 0, left, kd)
            far_block = q_ref[far] if q_index is None else q_ref[q_index, far]
            if row_ref is own:
                return own[left], far_block, own[mask]
            return row_ref[rr, left], far_block, row_ref[rr, mask]

        for w in range(0, 16, 2):
            l0, f0, m0 = pick(w)
            l1, f1, m1 = pick(w + 1)
            lhs = jnp.concatenate([l0, l1], axis=1)
            rhs = jnp.concatenate(
                [jnp.concatenate([f0, zero], axis=1), jnp.concatenate([zero, f1], axis=1)], axis=0
            )
            product = jnp.dot(lhs, rhs, preferred_element_type=jnp.float32)
            acc = acc + product[:, :size] * m0.astype(jnp.float32)
            acc = acc + product[:, size:] * m1.astype(jnp.float32)
        return acc

    row_groups = {
        "O": (own, lists_own, far_own, 0, 1),
        "N": (r_near, lists_near, far_near, 1, 3),
        "F": (r_far, lists_far, far_far, 4, 4),
    }
    src_groups = {
        "O": [(own, None, 0)],
        "N": [(q_near, o - 1, o) for o in (R, D, L)],
        "Z": [(q_zown, None, 4)],
        "F": [(q_far, o - 1, 4 + o) for o in (R, D, L)],
    }

    def work(rg, qgs):
        row_ref, lists, fars, slot0, count = row_groups[rg]

        def one(rr, carry):
            acc = accum[slot0 + rr]
            for qg in qgs:
                for q_ref, q_index, o in src_groups[qg]:
                    acc = triples(row_ref, lists, fars, rr, q_ref, q_index, source_group(o), acc)
            accum[slot0 + rr] = acc
            return carry

        if count == 1:
            one(0, 0)
        else:
            lax.fori_loop(0, count, one, 0)

    def forward(ring):
        ring["L"].wait_recv()
        ring["D1"].start()
        ring["R"].wait_recv()
        ring["D2"].start()

    work("O", ["O"])
    forward(rn)
    forward(qn)
    rz.wait_recv()
    rf["L"].start()
    rf["R"].start()

    moves = []
    for o in range(1, 8):
        dst_l = lists_near.at[o - 1] if o < 4 else lists_far.at[o - 4]
        dst_f = far_near.at[o - 1] if o < 4 else far_far.at[o - 4]
        remote(lists_hbm, lists_v.at[o], send_l.at[o], recv_l.at[o], row_at(z1, 0)).wait_recv()
        remote(far_hbm, far_v.at[o], send_f.at[o], recv_f.at[o], row_at(z1, 0)).wait_recv()
        moves.append(pltpu.make_async_copy(lists_v.at[o], dst_l, smem_sem.at[o]))
        moves.append(pltpu.make_async_copy(far_v.at[o], dst_f, smem_sem.at[8 + o]))
    for move in moves:
        move.start()
    for move in moves:
        move.wait()

    qz.wait_recv()
    qf["L"].start()
    qf["R"].start()
    forward(rf)
    for ring in (rn, qn):
        ring["D1"].wait_recv()
        ring["D2"].wait_recv()
    work("O", ["N", "Z"])
    work("N", ["O", "N", "Z"])
    forward(qf)
    rf["D1"].wait_recv()
    rf["D2"].wait_recv()
    work("F", ["O", "N", "Z"])
    qf["D1"].wait_recv()
    qf["D2"].wait_recv()
    for rg in ("O", "N", "F"):
        work(rg, ["F"])

    def row_of(s):
        return jnp.sum(jnp.transpose(accum[s]), axis=0, keepdims=True)

    whole_sum = row_of(0)
    part_recv[0] = whole_sum
    for o in range(1, 8):
        row = row_of(o)
        part_send[o] = row
        whole_sum = whole_sum + row
    plane_recv[place] = whole_sum
    part_send[0] = whole_sum

    def plane_copy(p):
        return remote(part_send.at[0], plane_recv.at[place], send_t.at[p], recv_t.at[place], plane_dev(p))

    def level_copy(p):
        return remote(depth_send, depth_recv.at[level], send_d.at[p], recv_d.at[level], level_dev(p))

    def plane_start(k, carry):
        plane_copy(lax.rem(place + k, 16)).start()
        return carry

    lax.fori_loop(1, 16, plane_start, 0)
    part_copies = []
    for o in range(1, 8):
        dev = row_at(z if o < 4 else z1, o % 4)
        there = (o // 4) * 4 + back[o % 4]
        part_copies.append(remote(part_send.at[o], part_recv.at[there], send_p.at[o], recv_p.at[there], dev))
    for copy in part_copies:
        copy.start()

    def plane_wait(k, carry):
        p = lax.rem(place + k, 16)
        remote(part_send.at[0], plane_recv.at[p], send_t.at[p], recv_t.at[p], plane_dev(p)).wait_recv()
        return carry

    lax.fori_loop(1, 16, plane_wait, 0)
    depth_sum = plane_recv[0]
    for p in range(1, 16):
        depth_sum = depth_sum + plane_recv[p]
    depth_send[...] = depth_sum
    depth_recv[level] = depth_sum

    def level_start(k, carry):
        level_copy(lax.rem(level + k, 16)).start()
        return carry

    lax.fori_loop(1, 16, level_start, 0)

    for o in range(1, 8):
        remote(part_send.at[o], part_recv.at[o], send_p.at[o], recv_p.at[o], row_at(z1, 0)).wait_recv()
    participation = part_recv[0]
    for o in range(1, 8):
        participation = participation + part_recv[o]
    part_ref[...] = participation

    def level_wait(k, carry):
        p = lax.rem(level + k, 16)
        remote(depth_send, depth_recv.at[p], send_d.at[p], recv_d.at[p], level_dev(p)).wait_recv()
        return carry

    lax.fori_loop(1, 16, level_wait, 0)
    grand = depth_recv[0]
    for p in range(1, 16):
        grand = grand + depth_recv[p]
    total_ref[...] = jnp.sum(grand, axis=1, keepdims=True) * (1.0 / math.sqrt(256 * size))

    for ring in (rn, qn, rf, qf):
        for copy in ring.values():
            copy.wait_send()
    rz.wait_send()
    qz.wait_send()
    for copy in list_copies + part_copies:
        copy.wait_send()

    def sent(k, carry):
        plane_copy(lax.rem(place + k, 16)).wait_send()
        level_copy(lax.rem(level + k, 16)).wait_send()
        return carry

    lax.fori_loop(1, 16, sent, 0)


def local(blocks, block_cols, far_slots, pair_lists):
    kd, size = blocks.shape[0], blocks.shape[1]
    lists = pair_lists[0]
    width = lists.shape[1]
    fars = far_slots.shape[1]
    block = (size, size)
    dma = pltpu.SemaphoreType.DMA
    smem = pltpu.SMEM
    vmem = pltpu.VMEM
    bf16, f32, i32 = jnp.bfloat16, jnp.float32, jnp.int32
    participation, total = pl.pallas_call(
        kernel,
        out_shape=(
            jax.ShapeDtypeStruct((1, size), f32),
            jax.ShapeDtypeStruct((1, 1), f32),
        ),
        in_specs=[
            pl.BlockSpec(memory_space=pl.ANY),
            pl.BlockSpec(memory_space=pltpu.SMEM),
            pl.BlockSpec(memory_space=pl.ANY),
            pl.BlockSpec(memory_space=pl.ANY),
        ],
        out_specs=(
            pl.BlockSpec(memory_space=pltpu.VMEM),
            pl.BlockSpec(memory_space=pltpu.VMEM),
        ),
        scratch_shapes=[
            vmem((kd,) + block, bf16),
            vmem((kd + 1,) + block, bf16),
            vmem((3, kd + 1) + block, bf16),
            vmem((4, kd + 1) + block, bf16),
            vmem((3, kd) + block, bf16),
            vmem((kd,) + block, bf16),
            vmem((3, kd) + block, bf16),
            vmem((8, 4, width), i32),
            vmem((8, 1, fars), i32),
            smem((1, 4, width), i32),
            smem((1, 1, fars), i32),
            smem((3, 4, width), i32),
            smem((3, 1, fars), i32),
            smem((4, 4, width), i32),
            smem((4, 1, fars), i32),
            vmem((8,) + block, f32),
            vmem((8, 1, size), f32),
            vmem((8, 1, size), f32),
            vmem((16, 1, size), f32),
            vmem((1, size), f32),
            vmem((16, 1, size), f32),
            dma((3,)),
            dma((16,)),
            dma((9,)), dma((9,)), dma((9,)), dma((9,)),
            dma((8,)), dma((8,)), dma((8,)), dma((8,)),
            dma((8,)), dma((8,)), dma((16,)), dma((16,)), dma((16,)), dma((16,)),
        ],
        compiler_params=pltpu.CompilerParams(
            collective_id=0, has_side_effects=True, vmem_limit_bytes=48 * 1024 * 1024
        ),
    )(blocks, block_cols, far_slots[:, None, :][0], pair_lists[0])
    return (participation.reshape(size), total.reshape(()))


def solution(mesh):
    torus = Mesh(mesh.devices.reshape(4, 4, 4, 2, 2), GRP_SUB)
    in_specs = (P(GRP_SUB, None, None), P(GRP_SUB), P(GRP_SUB, None), P(GRP_SUB, None, None))
    out_specs = (P(GRP_SUB), P())
    return jax.shard_map(local, mesh=torus, in_specs=in_specs, out_specs=out_specs, check_vma=False)
```

time: 507 us -> 62.4 us (0.12)
  waiting for transfers between devices: 192 us -> 0 us
  matrix products: 169 us -> 0 us
  local copies, waits for them, and re-layouts: 66.3 us -> 2.85 us
  Pallas kernels: 0 us -> 56.9 us
  blocking collectives: 48.5 us -> 0 us
  starting transfers between devices: 18.4 us -> 0 us
    all_to_all x2 -> x0, waiting for transfers between devices: 192 us -> none  [the longest x1 185 us: local(): lax.all_to_all(outgoing, GRP, split_axis=0, concat_axis=0, tiled=True)]
    dot_general x321 -> x0, matrix products: 169 us -> none  [the longest x193 127 us: select_rows(): jnp.dot(choices_of, table, preferred_element_type=jnp.float32)]
    pallas_call x0 -> x1, Pallas kernels: none -> 56.9 us  [local(): pl.pallas_call(kernel, out_shape=(jax.ShapeDtypeStruct((1, size), f32), j...]
    psum x5 -> x0, blocking collectives: 48.5 us -> none  [by_axis(): value = lax.psum(value, axis)]
    convert_element_type x65 -> x0, local copies, waits for them, and re-layouts: 38.4 us -> none  [the longest x64 21.2 us: triple_sums(): sums = jnp.sum(mask_blocks.astype(jnp.float32) * product, axis=2)]
    while x192 -> x0, local copies, waits for them, and re-layouts: 24.8 us -> none
    all_to_all x2 -> x0, starting transfers between devices: 18.4 us -> none  [the longest x1 12.5 us: local(): lax.all_to_all(wanted_row, GRP, split_axis=0, concat_axis=0, tiled=True)]
  transfers between devices with their start and end apart: 2 -> 0, of which waited for: 2 -> 0; matrix products, arithmetic and copies ran while one was open for 1% -> 0% of each run, Pallas kernels for 0% -> 0%
where the time goes in v1:
time: 62.4 us; the launch traced here: 62.2 us
  Pallas kernels  56.9 us (91%)
  local copies, waits for them, and re-layouts  2.85 us (5%)
  between operations  2.41 us (4%)
    pallas_call x1, Pallas kernels, local(): pl.pallas_call(kernel, out_shape=(jax.ShapeDtypeStruct((1, size), f32), j...  56.9 us
    unnamed x9, local copies, waits for them, and re-layouts  2.85 us

profile of v1, /device:TPU:1, one launch (start us, length us, event | category | flops | bytes accessed | tf_op | source)
XLA Modules:
  0.0 62.2 jit_solution(1835977422064619555)
XLA Ops:
  0.6 0.0 copy-start.2
  0.6 0.0 copy-start.3
  0.6 0.7 %copy-done.2 = s32[1,256]{1,0:T(1,128)S(1)} copy-done((s32[1,256]{1,0:T(1,128)S(1)}, s32[1,256]{1,0:T(1,128)}, u32[]{:S(2)}) %copy-start.2) | copy-done | bytes 1048
  1.3 0.0 copy-done.3
  1.3 0.0 copy-start
  1.3 0.9 %copy-done = bf16[8,128,128]{2,1,0:T(8,128)(2,1)S(1)} copy-done((bf16[8,128,128]{2,1,0:T(8,128)(2,1)S(1)}, bf16[8,128,128]{2,1,0:T(8,128)(2,1)}, u32[]{:S(2)}) %copy-start) | copy-done | bytes 262168
  2.3 0.0 copy-start.1
  2.3 0.7 %copy-done.1 = s32[1,4,1024]{2,1,0:T(4,128)S(1)} copy-done((s32[1,4,1024]{2,1,0:T(4,128)S(1)}, s32[1,4,1024]{2,1,0:T(4,128)}, u32[]{:S(2)}) %copy-start.1) | copy-done | bytes 16408
  3.0 56.9 %shard_map.59 = (f32[1,128]{1,0:T(1,128)S(1)}, f32[1,1]{1,0:T(1,128)}) custom-call(bf16[8,128,128]{2,1,0:T(8,128)(2,1)S(1)} %copy-done, s32[8]{0:T(128)S(1)} %copy-done.3, s32[1,256]{1,0:T(1,128)S(1)} %copy-done.2, s32[4,1024]{1,0:T(4,128)S(1)} %bitcast.3), custom_call_target="tpu_custom_call" | custom-call | tf_op jit(solution)/shard_map/pallas_call | solution.py:347
  59.9 0.5 copy.8
Async XLA Ops:
  0.6 0.7 %copy-start.2 = (s32[1,256]{1,0:T(1,128)S(1)}, s32[1,256]{1,0:T(1,128)}, u32[]{:S(2)}) copy-start(s32[1,256]{1,0:T(1,128)} %far_hbm.1) | copy-start | bytes 3076
  0.6 0.7 %copy-start.3 = (s32[8]{0:T(128)S(1)}, s32[8]{0:T(128)}, u32[]{:S(2)}) copy-start(s32[8]{0:T(128)} %cols_ref.1) | copy-start | bytes 100
  1.3 1.0 %copy-start = (bf16[8,128,128]{2,1,0:T(8,128)(2,1)S(1)}, bf16[8,128,128]{2,1,0:T(8,128)(2,1)}, u32[]{:S(2)}) copy-start(bf16[8,128,128]{2,1,0:T(8,128)(2,1)} %blocks_hbm.1) | copy-start | bytes 786436
  2.3 0.7 %copy-start.1 = (s32[1,4,1024]{2,1,0:T(4,128)S(1)}, s32[1,4,1024]{2,1,0:T(4,128)}, u32[]{:S(2)}) copy-start(s32[1,4,1024]{2,1,0:T(4,128)} %param.7) | copy-start | bytes 49156

commit v2 on v0

v2 whole, which is shorter than its diff:
```python
import functools
import math

import jax
import jax.numpy as jnp
from jax import lax
from jax.experimental import pallas as pl
from jax.experimental.pallas import tpu as pltpu
from jax.sharding import Mesh
from jax.sharding import PartitionSpec as P

GRP = ("grp_0", "grp_1", "grp_2")
SUB = ("sub_0", "sub_1")
GRP_SUB = GRP + SUB
MESH_IDS = pl.DeviceIdType.MESH
R, D, L = 1, 2, 3


def kernel(
    blocks_hbm, cols_hbm, far_hbm, lists_hbm,
    part_ref,
    raw, own, r_nlr, r_nd, r_zo, r_zlr, r_zd, q_nlr, q_nd, q_zo, q_zlr, q_zd,
    lists_v, far_v, lists_own, far_own, lists_near, far_near, lists_far, far_far, cols_s,
    accum, part_send, part_recv, plane_recv, depth_send, depth_recv,
    load_sem, smem_sem,
    send_r, recv_r, send_q, recv_q, send_l, recv_l, send_m, recv_m, send_f, recv_f,
    send_p, recv_p, send_t, recv_t, send_d, recv_d, tokens,
):
    z = lax.axis_index("grp_0")
    x = lax.axis_index("grp_1")
    y = lax.axis_index("grp_2")
    zh = lax.axis_index("sub_0")
    core = lax.axis_index("sub_1")
    kd, size = blocks_hbm.shape[0], blocks_hbm.shape[1]
    half, quarter = kd // 2, kd // 4
    oc, oh = 1 - core, 1 - zh
    z1 = z + 1 - 2 * lax.rem(z, 2)
    z2 = lax.rem(z + 2, 4)
    z3 = 3 - z
    xs = [x] + [lax.rem(x + o, 4) for o in (1, 2, 3)]
    ys = [y] + [lax.rem(y + o, 4) for o in (1, 2, 3)]
    back = (0, L, D, R)

    def row_at(zz, o):
        return (zz, x + core * (xs[o] - x), y + oc * (ys[o] - y), zh, core)

    def src_at(zz, o):
        return (zz, x + oc * (xs[o] - x), y + core * (ys[o] - y), zh, core)

    plane = [(dx, dy) for dx in range(4) for dy in range(4)][1:]
    depth = [(t, c, h) for t in range(4) for c in range(2) for h in range(2)][1:]
    place = x * 4 + y
    level = (zh * 4 + z) * 2 + core

    def plane_dev(k):
        dx, dy = plane[k]
        return (z, xs[dx], ys[dy], zh, core)

    def level_dev(k):
        t, c, h = depth[k]
        return ((z, z1, z2, z3)[t], x, y, (zh, oh)[h], (core, oc)[c])

    def local_copy(src, dst, sem):
        return pltpu.make_async_copy(src, dst, sem)

    def remote(src, dst, ssem, rsem, dev):
        return pltpu.make_async_remote_copy(
            src_ref=src, dst_ref=dst, send_sem=ssem, recv_sem=rsem,
            device_id=dev, device_id_type=MESH_IDS,
        )

    def columns(zz):
        return pl.ds(pl.multiple_of(zz * 256, 256), 256)

    barrier = pltpu.get_barrier_semaphore()
    load = local_copy(blocks_hbm, raw, load_sem.at[0])
    load.start()
    load_cols = local_copy(cols_hbm, cols_s, load_sem.at[1])
    load_cols.start()
    greeted = [row_at(z, o) for o in (R, D, L)] + [src_at(z, o) for o in (R, D, L)]
    greeted += [row_at(z1, o) for o in range(4)] + [src_at(z2, 0)]
    odd = lax.rem(z, 2)
    turned = lax.rem(z + 2 * odd + 3, 4)
    crossed = odd * (z // 3) + (1 - odd) * (1 - (z + 3) // 4)
    beyond = (turned, x, y, zh + crossed * (oh - zh), core)
    greeted += [(z, x, y, zh, oc), beyond]
    for dev in greeted:
        pl.semaphore_signal(barrier, inc=1, device_id=dev, device_id_type=MESH_IDS)
    own_moves = [
        local_copy(lists_hbm.at[:, columns(z)], lists_own.at[0, 0], load_sem.at[2]),
        local_copy(lists_hbm.at[:, columns(z2)], lists_own.at[0, 1], load_sem.at[3]),
        local_copy(far_hbm, far_own.at[0], load_sem.at[4]),
    ]
    for move in own_moves:
        move.start()

    zero = jnp.zeros((size, size), jnp.bfloat16)
    for ref, count in ((own, 0), (r_nlr, 2), (r_nd, 1), (r_zo, 1), (r_zlr, 2), (r_zd, 1)):
        for s in range(max(count, 1)):
            if count:
                ref[s, kd] = zero
            else:
                ref[kd] = zero
    for s in range(8):
        accum[s] = jnp.zeros((size, size), jnp.float32)
    load_cols.wait()
    load.wait()
    me = ((z * 4 + x) * 4 + y) * 4 + zh * 2 + core
    rows = lax.broadcasted_iota(jnp.int32, (size, size), 0)
    cols = lax.broadcasted_iota(jnp.int32, (size, size), 1)
    for t in range(kd):
        shift = jnp.where(cols_s[t] == me, 0, size)
        block = raw[t].astype(jnp.float32)
        own[t] = jnp.where(rows + shift > cols, block, 0.0).astype(jnp.bfloat16)

    pl.semaphore_wait(barrier, len(greeted))

    def token(k):
        for dev in (row_at(z1, 0), beyond):
            pl.semaphore_signal(tokens.at[k], inc=1, device_id=dev, device_id_type=MESH_IDS)

    def await_token(k):
        pl.semaphore_wait(tokens.at[k], 2)

    token(0)

    h1, h2 = pl.ds(0, half), pl.ds(half, half)

    def slot_r(o):
        return {R: r_nlr.at[0], L: r_nlr.at[1], D: r_nd.at[0], 4: r_zo.at[0],
                4 + R: r_zlr.at[0], 4 + L: r_zlr.at[1], 4 + D: r_zd.at[0]}[o]

    def slot_q(o):
        return {R: q_nlr.at[0], L: q_nlr.at[1], D: q_nd.at[0], 4: q_zo.at[0],
                4 + R: q_zlr.at[0], 4 + L: q_zlr.at[1], 4 + D: q_zd.at[0]}[o]

    def ring_copies(slot, src, dev, base, ssem, rsem, first_sem, parts, passed):
        right, left = dev(z, 1), dev(z, 3)
        ring, k = {}, first_sem
        for name, o, to in (("L", L, right), ("R", R, left)):
            for p, part in enumerate(parts):
                ring[name + str(p)] = remote(src.at[part], slot(base + o).at[part], ssem.at[k], rsem.at[k], to)
                k += 1
        for p, part in enumerate(parts):
            o, to = (L, right) if passed[p] in "Ll" else (R, left)
            via, to = (slot(base + o), to) if passed[p] in "LR" else (src, dev(z, D))
            ring["D" + str(p)] = remote(via.at[part], slot(base + D).at[part], ssem.at[k], rsem.at[k], to)
            k += 1
        return ring

    halves = (h1, h2)
    quarters = tuple(pl.ds(p * quarter, quarter) for p in range(4))
    rn = ring_copies(slot_r, own, row_at, 0, send_r, recv_r, 0, halves, "LR")
    qn = ring_copies(slot_q, own, src_at, 0, send_q, recv_q, 0, halves, "LR")
    rf = ring_copies(slot_r, slot_r(4), row_at, 4, send_r, recv_r, 6, quarters, "LRlr")
    qf = ring_copies(slot_q, slot_q(4), src_at, 4, send_q, recv_q, 6, quarters, "LRlr")
    rz = [remote(own.at[h], slot_r(4).at[h], send_r.at[18 + k], recv_r.at[18 + k], row_at(z1, 0)) for k, h in enumerate(quarters)]
    qz = [remote(own.at[h], slot_q(4).at[h], send_q.at[18 + k], recv_q.at[18 + k], src_at(z2, 0)) for k, h in enumerate(quarters)]

    for copy in rz + qz:
        copy.start()
    for ring in (rn, qn):
        ring["L0"].start()
        ring["R1"].start()
    for ring in (rn, qn):
        ring["L1"].start()
        ring["R0"].start()

    list_copies = []
    for o in range(1, 8):
        zz, zt = (z, z2) if o < 4 else (z1, z3)
        dev = row_at(zz, o % 4)
        there = (o // 4) * 4 + back[o % 4]
        list_copies.append(remote(lists_hbm.at[:, columns(zz)], lists_v.at[there, 0], send_l.at[o], recv_l.at[there], dev))
        list_copies.append(remote(lists_hbm.at[:, columns(zt)], lists_v.at[there, 1], send_m.at[o], recv_m.at[there], dev))
        list_copies.append(remote(far_hbm, far_v.at[there], send_f.at[o], recv_f.at[there], dev))
    for copy in list_copies:
        copy.start()

    ub = x + core * (y - x)
    ua = y + core * (x - y)

    def source_place(o):
        b = lax.rem(ub + o, 4)
        xq = b + core * (ua - b)
        yq = ua + core * (b - ua)
        return xq * 4 + yq

    def triples(row_ref, lists, fars, rr, o, acc):
        at_place = source_place(o % 4)
        base = at_place * 16
        far_base = (z if o < 4 else z2) * 64 + at_place * 4
        t = o // 4

        def pick(w):
            left = lists[rr, t, 0, base + w]
            far = fars[rr, 0, far_base + lists[rr, t, 1, base + w]]
            mask = lists[rr, t, 2, base + w]
            left = jnp.where(lists[rr, t, 3, base + w] > 0, left, kd)
            q_ref, q_index = {
                0: (own, None), R: (q_nlr, 0), L: (q_nlr, 1), D: (q_nd, 0), 4: (q_zo, 0),
                4 + R: (q_zlr, 0), 4 + L: (q_zlr, 1), 4 + D: (q_zd, 0),
            }[o]
            far_block = q_ref[far] if q_index is None else q_ref[q_index, far]
            if row_ref is own:
                return own[left], far_block, own[mask]
            at_row = 0 if row_ref is not r_nlr and row_ref is not r_zlr else rr_local
            return row_ref[at_row, left], far_block, row_ref[at_row, mask]

        rr_local = row_local[0]
        for w in range(0, 16, 2):
            l0, f0, m0 = pick(w)
            l1, f1, m1 = pick(w + 1)
            lhs = jnp.concatenate([l0, l1], axis=1)
            rhs = jnp.concatenate(
                [jnp.concatenate([f0, zero], axis=1), jnp.concatenate([zero, f1], axis=1)], axis=0
            )
            product = jnp.dot(lhs, rhs, preferred_element_type=jnp.float32)
            acc = acc + product[:, :size] * m0.astype(jnp.float32)
            acc = acc + product[:, size:] * m1.astype(jnp.float32)
        return acc

    row_local = [0]
    row_groups = {
        "O": (own, lists_own, far_own, (0,), (0,)),
        "LR": (r_nlr, lists_near, far_near, (R, L), (0, 2)),
        "D": (r_nd, lists_near, far_near, (D,), (1,)),
        "zO": (r_zo, lists_far, far_far, (4,), (0,)),
        "zLR": (r_zlr, lists_far, far_far, (4 + R, 4 + L), (1, 3)),
        "zD": (r_zd, lists_far, far_far, (4 + D,), (2,)),
    }
    sources = {"O": (0,), "LR": (R, L), "D": (D,), "zO": (4,), "zLR": (4 + R, 4 + L), "zD": (4 + D,)}

    def work(rgs, qgs):
        for rg in rgs:
            row_ref, lists, fars, slots, at_list = row_groups[rg]

            def one(k, carry):
                row_local[0] = k
                slot = slots[0] if len(slots) == 1 else slots[0] + 2 * k
                rr = at_list[0] if len(slots) == 1 else at_list[0] + 2 * k
                acc = accum[slot]
                for qg in qgs:
                    for o in sources[qg]:
                        acc = triples(row_ref, lists, fars, rr, o, acc)
                accum[slot] = acc
                return carry

            if len(slots) == 1:
                one(0, 0)
            else:
                for k in range(len(slots)):
                    one(k, 0)

    def list_moves(slots):
        moves = []
        for o in slots:
            k, dst_l, dst_f = (o - 1, lists_near, far_near) if o < 4 else (o - 4, lists_far, far_far)
            dev = row_at(z1, 0)
            remote(lists_hbm.at[:, columns(z)], lists_v.at[o, 0], send_l.at[o], recv_l.at[o], dev).wait_recv()
            remote(lists_hbm.at[:, columns(z)], lists_v.at[o, 1], send_m.at[o], recv_m.at[o], dev).wait_recv()
            remote(far_hbm, far_v.at[o], send_f.at[o], recv_f.at[o], dev).wait_recv()
            moves.append(local_copy(lists_v.at[o], dst_l.at[k], smem_sem.at[o]))
            moves.append(local_copy(far_v.at[o], dst_f.at[k], smem_sem.at[8 + o]))
        for move in moves:
            move.start()
        return moves

    def finish(moves):
        for move in moves:
            move.wait()

    def got(ring, *names):
        for name in names:
            ring[name].wait_recv()

    def spread(zcopies, ring, *parts):
        for p in parts:
            zcopies[p].wait_recv()
            if p > 1:
                ring["D" + str(p)].start()
            ring["L" + str(p)].start()
            ring["R" + str(p)].start()

    def relay(ring, *names):
        for name in names:
            ring[name].wait_recv()
            ring["D" + name[1]].start()

    finish(own_moves)
    work(["O"], ["O"])
    await_token(0)
    token(1)
    relay(rn, "L0", "R1")
    relay(qn, "L0", "R1")
    spread(rz, rf, 0, 1)
    await_token(1)
    token(2)
    got(rn, "L1", "R0")
    got(qn, "L1", "R0")
    finish(list_moves((1, 2, 3)))
    work(["O"], ["LR"])
    spread(rz, rf, 2, 3)
    spread(qz, qf, 0)
    work(["LR"], ["O", "LR"])
    relay(rf, "L0", "R1")
    spread(qz, qf, 1)
    got(rn, "D0", "D1")
    got(qn, "D0", "D1")
    work(["O", "LR"], ["D"])
    spread(qz, qf, 2)
    work(["D"], ["O", "LR", "D"])
    relay(qf, "L0", "R1")
    await_token(2)
    finish(list_moves((4, 5, 6, 7)))
    work(["zO"], ["O", "LR", "D"])
    spread(qz, qf, 3)
    got(rf, "R0", "L1", "L2", "R2", "L3", "R3")
    work(["zLR"], ["O", "LR", "D"])
    work(["O", "LR", "D", "zO", "zLR"], ["zO"])
    got(rf, "D0", "D1", "D2", "D3")
    work(["zD"], ["O", "LR", "D", "zO"])
    got(qf, "R0", "L1", "L2", "R2", "L3", "R3")
    work(["O", "LR", "D", "zO", "zLR", "zD"], ["zLR"])
    got(qf, "D0", "D1", "D2", "D3")
    work(["O", "LR", "D", "zO", "zLR", "zD"], ["zD"])

    def row_of(s):
        return jnp.sum(jnp.transpose(accum[s]), axis=0, keepdims=True)

    partials = [row_of(s) for s in range(8)]
    whole_sum = partials[0]
    for s in range(1, 8):
        part_send[s] = partials[s]
        whole_sum = whole_sum + partials[s]
    part_send[0] = whole_sum
    plane_recv[place] = whole_sum
    part_recv[0] = partials[0]

    def plane_there(k):
        dx, dy = plane[k]
        return plane.index(((4 - dx) % 4, (4 - dy) % 4))

    plane_copies = [
        remote(part_send.at[0], plane_recv.at[place], send_t.at[k], recv_t.at[plane_there(k)], plane_dev(k))
        for k in range(15)
    ]
    for copy in plane_copies:
        copy.start()
    part_copies = []
    for o in range(1, 8):
        dev = row_at(z if o < 4 else z1, o % 4)
        there = (o // 4) * 4 + back[o % 4]
        part_copies.append(remote(part_send.at[o], part_recv.at[there], send_p.at[o], recv_p.at[there], dev))
    for copy in part_copies:
        copy.start()

    for o in range(1, 8):
        remote(part_send.at[o], part_recv.at[o], send_p.at[o], recv_p.at[o], row_at(z1, 0)).wait_recv()
    for k in range(15):
        remote(part_send.at[0], plane_recv.at[place], send_t.at[k], recv_t.at[k], plane_dev(k)).wait_recv()
    depth_sum = plane_recv[0]
    for p in range(1, 16):
        depth_sum = depth_sum + plane_recv[p]
    depth_send[...] = depth_sum
    depth_recv[level] = depth_sum
    level_copies = [
        remote(depth_send, depth_recv.at[level], send_d.at[k], recv_d.at[k], level_dev(k)) for k in range(15)
    ]
    for copy in level_copies:
        copy.start()
    participation = part_recv[0]
    for o in range(1, 8):
        participation = participation + part_recv[o]
    part_ref[0:1] = participation

    for ring in (rn, qn, rf, qf):
        for copy in ring.values():
            copy.wait_send()
    for copy in rz + qz + list_copies + part_copies + plane_copies:
        copy.wait_send()
    for copy in level_copies:
        copy.wait_recv()
    grand = depth_recv[0]
    for p in range(1, 16):
        grand = grand + depth_recv[p]
    part_ref[1:2] = jnp.broadcast_to(jnp.sum(grand, axis=1, keepdims=True) * (1.0 / math.sqrt(256 * size)), (1, size))
    for copy in level_copies:
        copy.wait_send()


def local(blocks, block_cols, far_slots, pair_lists):
    kd, size = blocks.shape[0], blocks.shape[1]
    fars = far_slots.shape[1]
    block = (size, size)
    dma = pltpu.SemaphoreType.DMA
    smem = pltpu.SMEM
    vmem = pltpu.VMEM
    bf16, f32, i32 = jnp.bfloat16, jnp.float32, jnp.int32
    result = pl.pallas_call(
        kernel,
        out_shape=jax.ShapeDtypeStruct((2, size), f32),
        in_specs=[pl.BlockSpec(memory_space=pl.ANY)] * 4,
        out_specs=pl.BlockSpec(memory_space=pltpu.VMEM),
        scratch_shapes=[
            vmem((kd,) + block, bf16),
            vmem((kd + 1,) + block, bf16),
            vmem((2, kd + 1) + block, bf16),
            vmem((1, kd + 1) + block, bf16),
            vmem((1, kd + 1) + block, bf16),
            vmem((2, kd + 1) + block, bf16),
            vmem((1, kd + 1) + block, bf16),
            vmem((2, kd) + block, bf16),
            vmem((1, kd) + block, bf16),
            vmem((1, kd) + block, bf16),
            vmem((2, kd) + block, bf16),
            vmem((1, kd) + block, bf16),
            vmem((8, 2, 4, 256), i32),
            vmem((8, 1, fars), i32),
            smem((1, 2, 4, 256), i32),
            smem((1, 1, fars), i32),
            smem((3, 2, 4, 256), i32),
            smem((3, 1, fars), i32),
            smem((4, 2, 4, 256), i32),
            smem((4, 1, fars), i32),
            smem((kd,), i32),
            vmem((8,) + block, f32),
            vmem((8, 1, size), f32),
            vmem((8, 1, size), f32),
            vmem((16, 1, size), f32),
            vmem((1, size), f32),
            vmem((16, 1, size), f32),
            dma((5,)),
            dma((16,)),
            dma((22,)), dma((22,)), dma((22,)), dma((22,)),
            dma((8,)), dma((8,)), dma((8,)), dma((8,)), dma((8,)), dma((8,)),
            dma((8,)), dma((8,)), dma((15,)), dma((15,)), dma((15,)), dma((15,)),
            pltpu.SemaphoreType.REGULAR((3,)),
        ],
        compiler_params=pltpu.CompilerParams(
            collective_id=0, has_side_effects=True, vmem_limit_bytes=60 * 1024 * 1024
        ),
    )(blocks, block_cols, far_slots, pair_lists[0])
    return (result[0], result[1, 0])


def solution(mesh):
    torus = Mesh(mesh.devices.reshape(4, 4, 4, 2, 2), GRP_SUB)
    in_specs = (P(GRP_SUB, None, None), P(GRP_SUB), P(GRP_SUB, None), P(GRP_SUB, None, None))
    out_specs = (P(GRP_SUB), P())
    return jax.shard_map(local, mesh=torus, in_specs=in_specs, out_specs=out_specs, check_vma=False)
```

time: 507 us -> 54.3 us (0.11)
  waiting for transfers between devices: 192 us -> 0 us
  matrix products: 169 us -> 0 us
  local copies, waits for them, and re-layouts: 66.3 us -> 2.34 us
  Pallas kernels: 0 us -> 51.2 us
  blocking collectives: 48.5 us -> 0 us
  starting transfers between devices: 18.4 us -> 0 us
    all_to_all x2 -> x0, waiting for transfers between devices: 192 us -> none  [the longest x1 185 us: local(): lax.all_to_all(outgoing, GRP, split_axis=0, concat_axis=0, tiled=True)]
    dot_general x321 -> x0, matrix products: 169 us -> none  [the longest x193 127 us: select_rows(): jnp.dot(choices_of, table, preferred_element_type=jnp.float32)]
    pallas_call x0 -> x1, Pallas kernels: none -> 51.2 us  [local(): pl.pallas_call(kernel, out_shape=jax.ShapeDtypeStruct((2, size), f32), in...]
    psum x5 -> x0, blocking collectives: 48.5 us -> none  [by_axis(): value = lax.psum(value, axis)]
    convert_element_type x65 -> x0, local copies, waits for them, and re-layouts: 38.4 us -> none  [the longest x64 21.2 us: triple_sums(): sums = jnp.sum(mask_blocks.astype(jnp.float32) * product, axis=2)]
    while x192 -> x0, local copies, waits for them, and re-layouts: 24.8 us -> none
    all_to_all x2 -> x0, starting transfers between devices: 18.4 us -> none  [the longest x1 12.5 us: local(): lax.all_to_all(wanted_row, GRP, split_axis=0, concat_axis=0, tiled=True)]
  transfers between devices with their start and end apart: 2 -> 0, of which waited for: 2 -> 0; matrix products, arithmetic and copies ran while one was open for 1% -> 0% of each run, Pallas kernels for 0% -> 0%
where the time goes in v2:
time: 54.3 us; the launch traced here: 54.2 us
  Pallas kernels  51.2 us (94%)
  local copies, waits for them, and re-layouts  2.34 us (4%)
  between operations  0.64 us (1%)
    pallas_call x1, Pallas kernels, local(): pl.pallas_call(kernel, out_shape=jax.ShapeDtypeStruct((2, size), f32), in...  51.2 us
    slice x1, local copies, waits for them, and re-layouts, local(): return (result[0], result[1, 0])  1.17 us

profile of v2, /device:TPU:1, one launch (start us, length us, event | category | flops | bytes accessed | tf_op | source)
XLA Modules:
  0.0 54.2 jit_solution(16907331085278638719)
XLA Ops:
  0.6 51.2 %shard_map.59 = f32[2,128]{1,0:T(2,128)} custom-call(bf16[8,128,128]{2,1,0:T(8,128)(2,1)} %blocks_hbm.1, s32[8]{0:T(128)} %cols_hbm.1, s32[1,256]{1,0:T(1,128)} %far_hbm.1, s32[4,1024]{1,0:T(4,128)} %bitcast.4), custom_call_target="tpu_custom_call" | custom-call | tf_op jit(solution)/shard_map/pallas_call | solution.py:400
  51.8 1.2 %slice.7 = f32[1,1]{1,0:T(1,128)} slice(f32[2,128]{1,0:T(2,128)} %shard_map.59), slice={[1:2], [0:1]} | slice | bytes 8 | tf_op jit(solution)/shard_map/slice | solution.py:444
  53.0 0.0 copy-start
  53.0 0.7 %copy-done = f32[2,128]{1,0:T(2,128)S(1)} copy-done((f32[2,128]{1,0:T(2,128)S(1)}, f32[2,128]{1,0:T(2,128)}, u32[]{:S(2)}) %copy-start) | copy-done | bytes 1048
  53.7 0.5 slice_bitcast_fusion
Async XLA Ops:
  53.0 0.7 %copy-start = (f32[2,128]{1,0:T(2,128)S(1)}, f32[2,128]{1,0:T(2,128)}, u32[]{:S(2)}) copy-start(f32[2,128]{1,0:T(2,128)} %shard_map.59) | copy-start | bytes 3076

commit v3 on v2

--- a/solution.py
+++ b/solution.py
@@ -157,7 +157,14 @@
     rz = [remote(own.at[h], slot_r(4).at[h], send_r.at[18 + k], recv_r.at[18 + k], row_at(z1, 0)) for k, h in enumerate(quarters)]
     qz = [remote(own.at[h], slot_q(4).at[h], send_q.at[18 + k], recv_q.at[18 + k], src_at(z2, 0)) for k, h in enumerate(quarters)]
 
-    for copy in rz + qz:
+    middle = (z + 1) // 2 == 1
+
+    def start_outer():
+        for copy in rz:
+            copy.start()
+
+    pl.when(jnp.logical_not(middle))(start_outer)
+    for copy in qz:
         copy.start()
     for ring in (rn, qn):
         ring["L0"].start()
@@ -248,6 +255,8 @@
 
             if len(slots) == 1:
                 one(0, 0)
+            elif sum(len(sources[qg]) for qg in qgs) > 3:
+                lax.fori_loop(0, len(slots), one, 0)
             else:
                 for k in range(len(slots)):
                     one(k, 0)
@@ -277,65 +286,95 @@
     def spread(zcopies, ring, *parts):
         for p in parts:
             zcopies[p].wait_recv()
+            ring["L" + str(p)].start()
+            ring["R" + str(p)].start()
             if p > 1:
                 ring["D" + str(p)].start()
-            ring["L" + str(p)].start()
-            ring["R" + str(p)].start()
 
     def relay(ring, *names):
         for name in names:
             ring[name].wait_recv()
             ring["D" + name[1]].start()
 
+    def by_level(run):
+        pl.when(middle)(lambda: run(True))
+        pl.when(jnp.logical_not(middle))(lambda: run(False))
+
+    near = ["O", "LR", "D"]
+
+    def kinds(mid):
+        return ((rz, rf), (qz, qf)) if mid else ((qz, qf), (rz, rf))
+
+    def early(mid, first, others):
+        if mid:
+            work(first, others)
+        else:
+            work(others, first)
+
+    def late(mid, second, others):
+        early(not mid, second, others)
+
+    def begin(mid):
+        if mid:
+            for copy in rz:
+                copy.start()
+        spread(*kinds(mid)[0], 0, 1)
+
+    def turn(mid):
+        relay(kinds(mid)[0][1], "L0", "R1")
+        spread(*kinds(mid)[1], 0)
+
+    def last(mid):
+        (_, ring1), (z_second, ring2) = kinds(mid)
+        spread(z_second, ring2, 1)
+        finish(list_moves((4, 5, 6, 7)))
+        early(mid, ["zO"], near)
+        spread(z_second, ring2, 2)
+        relay(ring2, "L0")
+        got(ring1, "R0", "L1", "L2", "R2", "L3", "R3")
+        early(mid, ["zLR"], near)
+        spread(z_second, ring2, 3)
+        relay(ring2, "R1")
+        late(mid, ["zO"], near + ["zO", "zLR"])
+        got(ring1, "D0", "D1", "D2", "D3")
+        early(mid, ["zD"], near + ["zO"])
+        got(ring2, "R0", "L1", "L2", "R2", "L3", "R3")
+        late(mid, ["zLR"], near + ["zO", "zLR", "zD"])
+        got(ring2, "D0", "D1", "D2", "D3")
+        late(mid, ["zD"], near + ["zO", "zLR", "zD"])
+
     finish(own_moves)
     work(["O"], ["O"])
+    relay(rn, "L0", "R1")
+    relay(qn, "L0", "R1")
+    by_level(begin)
     await_token(0)
     token(1)
-    relay(rn, "L0", "R1")
-    relay(qn, "L0", "R1")
-    spread(rz, rf, 0, 1)
-    await_token(1)
-    token(2)
     got(rn, "L1", "R0")
     got(qn, "L1", "R0")
     finish(list_moves((1, 2, 3)))
+    by_level(lambda mid: spread(*kinds(mid)[0], 2))
     work(["O"], ["LR"])
-    spread(rz, rf, 2, 3)
-    spread(qz, qf, 0)
+    by_level(lambda mid: spread(*kinds(mid)[0], 3))
     work(["LR"], ["O", "LR"])
-    relay(rf, "L0", "R1")
-    spread(qz, qf, 1)
+    await_token(1)
+    token(2)
+    by_level(turn)
     got(rn, "D0", "D1")
     got(qn, "D0", "D1")
     work(["O", "LR"], ["D"])
-    spread(qz, qf, 2)
-    work(["D"], ["O", "LR", "D"])
-    relay(qf, "L0", "R1")
+    work(["D"], near)
     await_token(2)
-    finish(list_moves((4, 5, 6, 7)))
-    work(["zO"], ["O", "LR", "D"])
-    spread(qz, qf, 3)
-    got(rf, "R0", "L1", "L2", "R2", "L3", "R3")
-    work(["zLR"], ["O", "LR", "D"])
-    work(["O", "LR", "D", "zO", "zLR"], ["zO"])
-    got(rf, "D0", "D1", "D2", "D3")
-    work(["zD"], ["O", "LR", "D", "zO"])
-    got(qf, "R0", "L1", "L2", "R2", "L3", "R3")
-    work(["O", "LR", "D", "zO", "zLR", "zD"], ["zLR"])
-    got(qf, "D0", "D1", "D2", "D3")
-    work(["O", "LR", "D", "zO", "zLR", "zD"], ["zD"])
-
-    def row_of(s):
-        return jnp.sum(jnp.transpose(accum[s]), axis=0, keepdims=True)
-
-    partials = [row_of(s) for s in range(8)]
-    whole_sum = partials[0]
+    token(3)
+    by_level(last)
+    await_token(3)
+
+    mass = accum[0]
     for s in range(1, 8):
-        part_send[s] = partials[s]
-        whole_sum = whole_sum + partials[s]
+        mass = mass + accum[s]
+    whole_sum = jnp.sum(mass, axis=0, keepdims=True)
     part_send[0] = whole_sum
     plane_recv[place] = whole_sum
-    part_recv[0] = partials[0]
 
     def plane_there(k):
         dx, dy = plane[k]
@@ -347,6 +386,12 @@
     ]
     for copy in plane_copies:
         copy.start()
+
+    def row_of(s):
+        return jnp.sum(jnp.transpose(accum[s]), axis=0, keepdims=True)
+
+    for s in range(1, 8):
+        part_send[s] = row_of(s)
     part_copies = []
     for o in range(1, 8):
         dev = row_at(z if o < 4 else z1, o % 4)
@@ -355,8 +400,6 @@
     for copy in part_copies:
         copy.start()
 
-    for o in range(1, 8):
-        remote(part_send.at[o], part_recv.at[o], send_p.at[o], recv_p.at[o], row_at(z1, 0)).wait_recv()
     for k in range(15):
         remote(part_send.at[0], plane_recv.at[place], send_t.at[k], recv_t.at[k], plane_dev(k)).wait_recv()
     depth_sum = plane_recv[0]
@@ -369,7 +412,9 @@
     ]
     for copy in level_copies:
         copy.start()
-    participation = part_recv[0]
+    participation = row_of(0)
+    for o in range(1, 8):
+        remote(part_send.at[o], part_recv.at[o], send_p.at[o], recv_p.at[o], row_at(z1, 0)).wait_recv()
     for o in range(1, 8):
         participation = participation + part_recv[o]
     part_ref[0:1] = participation
@@ -435,7 +480,7 @@
             dma((22,)), dma((22,)), dma((22,)), dma((22,)),
             dma((8,)), dma((8,)), dma((8,)), dma((8,)), dma((8,)), dma((8,)),
             dma((8,)), dma((8,)), dma((15,)), dma((15,)), dma((15,)), dma((15,)),
-            pltpu.SemaphoreType.REGULAR((3,)),
+            pltpu.SemaphoreType.REGULAR((4,)),
         ],
         compiler_params=pltpu.CompilerParams(
             collective_id=0, has_side_effects=True, vmem_limit_bytes=60 * 1024 * 1024

time: 54.3 us -> 52.4 us (0.965)
  Pallas kernels: 51.2 us -> 49.3 us
    pallas_call x1, Pallas kernels: 51.2 us -> 49.3 us  [local(): pl.pallas_call(kernel, out_shape=jax.ShapeDtypeStruct((2, size), f32), in...]
where the time goes in v3:
time: 52.4 us; the launch traced here: 52.2 us
  Pallas kernels  49.3 us (94%)
  local copies, waits for them, and re-layouts  2.34 us (4%)
  between operations  0.64 us (1%)
    pallas_call x1, Pallas kernels, local(): pl.pallas_call(kernel, out_shape=jax.ShapeDtypeStruct((2, size), f32), in...  49.3 us
    slice x1, local copies, waits for them, and re-layouts, local(): return (result[0], result[1, 0])  1.17 us

profile of v3, /device:TPU:1, one launch (start us, length us, event | category | flops | bytes accessed | tf_op | source)
XLA Modules:
  0.0 52.2 jit_solution(571174396237647078)
XLA Ops:
  0.6 49.3 %shard_map.59 = f32[2,128]{1,0:T(2,128)} custom-call(bf16[8,128,128]{2,1,0:T(8,128)(2,1)} %blocks_hbm.1, s32[8]{0:T(128)} %cols_hbm.1, s32[1,256]{1,0:T(1,128)} %far_hbm.1, s32[4,1024]{1,0:T(4,128)} %bitcast.4), custom_call_target="tpu_custom_call" | custom-call | tf_op jit(solution)/shard_map/pallas_call | solution.py:445
  49.9 1.2 %slice.7 = f32[1,1]{1,0:T(1,128)} slice(f32[2,128]{1,0:T(2,128)} %shard_map.59), slice={[1:2], [0:1]} | slice | bytes 8 | tf_op jit(solution)/shard_map/slice | solution.py:489
  51.1 0.0 copy-start
  51.1 0.7 %copy-done = f32[2,128]{1,0:T(2,128)S(1)} copy-done((f32[2,128]{1,0:T(2,128)S(1)}, f32[2,128]{1,0:T(2,128)}, u32[]{:S(2)}) %copy-start) | copy-done | bytes 1048
  51.7 0.5 slice_bitcast_fusion
Async XLA Ops:
  51.1 0.7 %copy-start = (f32[2,128]{1,0:T(2,128)S(1)}, f32[2,128]{1,0:T(2,128)}, u32[]{:S(2)}) copy-start(f32[2,128]{1,0:T(2,128)} %shard_map.59) | copy-start | bytes 3076

commit v4 on v3

--- a/solution.py
+++ b/solution.py
@@ -152,8 +152,8 @@
     quarters = tuple(pl.ds(p * quarter, quarter) for p in range(4))
     rn = ring_copies(slot_r, own, row_at, 0, send_r, recv_r, 0, halves, "LR")
     qn = ring_copies(slot_q, own, src_at, 0, send_q, recv_q, 0, halves, "LR")
-    rf = ring_copies(slot_r, slot_r(4), row_at, 4, send_r, recv_r, 6, quarters, "LRlr")
-    qf = ring_copies(slot_q, slot_q(4), src_at, 4, send_q, recv_q, 6, quarters, "LRlr")
+    rf = ring_copies(slot_r, slot_r(4), row_at, 4, send_r, recv_r, 6, quarters, "Lrlr")
+    qf = ring_copies(slot_q, slot_q(4), src_at, 4, send_q, recv_q, 6, quarters, "Lrlr")
     rz = [remote(own.at[h], slot_r(4).at[h], send_r.at[18 + k], recv_r.at[18 + k], row_at(z1, 0)) for k, h in enumerate(quarters)]
     qz = [remote(own.at[h], slot_q(4).at[h], send_q.at[18 + k], recv_q.at[18 + k], src_at(z2, 0)) for k, h in enumerate(quarters)]
 
@@ -288,7 +288,7 @@
             zcopies[p].wait_recv()
             ring["L" + str(p)].start()
             ring["R" + str(p)].start()
-            if p > 1:
+            if p > 0:
                 ring["D" + str(p)].start()
 
     def relay(ring, *names):
@@ -321,7 +321,8 @@
         spread(*kinds(mid)[0], 0, 1)
 
     def turn(mid):
-        relay(kinds(mid)[0][1], "L0", "R1")
+        (relay if True else got)(kinds(mid)[0][1], "L0")
+        got(kinds(mid)[0][1], "R1")
         spread(*kinds(mid)[1], 0)
 
     def last(mid):
@@ -334,7 +335,7 @@
         got(ring1, "R0", "L1", "L2", "R2", "L3", "R3")
         early(mid, ["zLR"], near)
         spread(z_second, ring2, 3)
-        relay(ring2, "R1")
+        got(ring2, "R1")
         late(mid, ["zO"], near + ["zO", "zLR"])
         got(ring1, "D0", "D1", "D2", "D3")
         early(mid, ["zD"], near + ["zO"])

time: 52.4 us -> 52.9 us (level)
  no operation moved by 1% of the time
where the time goes in v4:
time: 52.9 us; the launch traced here: 52.7 us
  Pallas kernels  49.8 us (94%)
  local copies, waits for them, and re-layouts  2.34 us (4%)
  between operations  0.64 us (1%)
    pallas_call x1, Pallas kernels, local(): pl.pallas_call(kernel, out_shape=jax.ShapeDtypeStruct((2, size), f32), in...  49.8 us
    slice x1, local copies, waits for them, and re-layouts, local(): return (result[0], result[1, 0])  1.17 us

profile of v4, /device:TPU:1, one launch (start us, length us, event | category | flops | bytes accessed | tf_op | source)
XLA Modules:
  0.0 52.7 jit_solution(9115729261955902005)
XLA Ops:
  0.6 49.8 %shard_map.59 = f32[2,128]{1,0:T(2,128)} custom-call(bf16[8,128,128]{2,1,0:T(8,128)(2,1)} %blocks_hbm.1, s32[8]{0:T(128)} %cols_hbm.1, s32[1,256]{1,0:T(1,128)} %far_hbm.1, s32[4,1024]{1,0:T(4,128)} %bitcast.4), custom_call_target="tpu_custom_call" | custom-call | tf_op jit(solution)/shard_map/pallas_call | solution.py:446
  50.4 1.2 %slice.7 = f32[1,1]{1,0:T(1,128)} slice(f32[2,128]{1,0:T(2,128)} %shard_map.59), slice={[1:2], [0:1]} | slice | bytes 8 | tf_op jit(solution)/shard_map/slice | solution.py:490
  51.6 0.0 copy-start
  51.6 0.7 %copy-done = f32[2,128]{1,0:T(2,128)S(1)} copy-done((f32[2,128]{1,0:T(2,128)S(1)}, f32[2,128]{1,0:T(2,128)}, u32[]{:S(2)}) %copy-start) | copy-done | bytes 1048
  52.2 0.5 slice_bitcast_fusion
Async XLA Ops:
  51.6 0.7 %copy-start = (f32[2,128]{1,0:T(2,128)S(1)}, f32[2,128]{1,0:T(2,128)}, u32[]{:S(2)}) copy-start(f32[2,128]{1,0:T(2,128)} %shard_map.59) | copy-start | bytes 3076
